TPU v7x, 32 devices: a whole 2x2x4 slice. The times are simulated.
32 devices in a mesh: corpus: 16 (over z, y, x), batch: 2 (over core).
Axes of the slice: x: 2, y: 2, z: 4, core: 2. Of those that a mesh axis runs over, the one named last changes fastest.
Arguments:
- queries: float32 [128, 1024], P(('corpus', 'batch')), may hold values from -6.25 to 6.25, as said below
- codes: int32 [98304, 32], P('corpus'), may hold values from -2147483648 to 2147483647
- quant_rows: bfloat16 [98304, 1024], P('corpus'), may hold values from -127 to 127, as said below
- row_scale: float32 [98304], P('corpus'), may hold values from 0.0005 to 0.002
- candidates: int32 [128, 40], P(('corpus', 'batch')), may hold values from 0 to 98303
- shortlist: int32 [128], P(('corpus', 'batch')), may hold values from 1 to 40
- edges: int32 [17], replicated, may hold values from 464 to 563, as said below
Outputs:
- hist: float32 [128, 16], P(('corpus', 'batch'))
- scores: float32 [128, 40], P(('corpus', 'batch'))
Inputs may be any that keep to these rules, and one draw needn't show every extreme that they name: `queries`: no entry lies within 0.25 of zero. `quant_rows`: whole numbers. `edges`: strictly increasing.
All inputs are finite; a program needn't handle non-finite values.
Results may differ from a plain program's by a relative error of at most 0.0003.
Values sent between devices are 32-bit elements; how exact they have to be, the bound alone decides.
A program may use at most 64 MiB of HBM per device.

v0:
```python
import math

import jax
import jax.numpy as jnp
from jax import lax
from jax.sharding import PartitionSpec as P


def unpack(words):
    bits = jnp.right_shift(words[..., None], jnp.arange(32, dtype=jnp.int32)) & 1
    signed = (2 * bits - 1).reshape(words.shape[:-1] + (words.shape[-1] * 32,))
    return signed.astype(jnp.bfloat16)


def histogram(queries, codes, edges, width):
    count_q = queries.shape[0]
    count_rows = codes.shape[0]
    signs = jnp.where(queries >= 0, 1.0, -1.0).astype(jnp.bfloat16)
    limits = edges.astype(jnp.float32)
    block = math.gcd(count_rows, 1024)

    def step(total, number):
        words = lax.dynamic_slice_in_dim(codes, number * block, block, 0)
        plus = unpack(words)
        inner = jnp.dot(signs, plus.T, preferred_element_type=jnp.float32)
        ham = (width - inner) * 0.5
        above = jnp.stack(
            [
                jnp.sum((ham >= limits[k]).astype(jnp.float32), axis=1)
                for k in range(limits.shape[0])
            ],
            axis=1,
        )
        return (total + above, None)

    start_total = jnp.zeros((count_q, limits.shape[0]), jnp.float32)
    above, _ = lax.scan(step, start_total, jnp.arange(count_rows // block, dtype=jnp.int32))
    return above[:, :-1] - above[:, 1:]


def rescore(queries, quant_rows, row_scale, lists, lengths, base, first, span):
    count_rows = quant_rows.shape[0]
    count_q, cand = lists.shape
    total_slots = count_q * cand
    group = 512
    local = lists - base
    slot_ids = jnp.arange(cand, dtype=jnp.int32)
    live = (local >= first) & (local < first + span) & (slot_ids[None, :] < lengths[:, None])
    flat_live = live.reshape(-1)
    flat_target = jnp.clip(local, 0, count_rows - 1).reshape(-1)
    rank = jnp.cumsum(flat_live.astype(jnp.int32)) - 1
    place = jnp.where(flat_live, rank, total_slots + group)
    order = (
        jnp.zeros((total_slots + group,), jnp.int32)
        .at[place]
        .set(jnp.arange(total_slots, dtype=jnp.int32), mode="drop")
    )
    found = jnp.sum(flat_live.astype(jnp.int32))
    trips = (found + group - 1) // group
    lanes = jnp.arange(group, dtype=jnp.int32)

    def visit(number, flat_scores):
        picked = lax.dynamic_slice_in_dim(order, number * group, group, 0)
        valid = number * group + lanes < found
        owner = picked // cand
        target = flat_target[picked]
        values = (
            jnp.sum(queries[owner] * quant_rows[target].astype(jnp.float32), axis=1)
            * row_scale[target]
        )
        spot = jnp.where(valid, picked, total_slots)
        return flat_scores.at[spot].set(values, mode="drop")

    flat = lax.fori_loop(0, trips, visit, jnp.zeros((total_slots,), jnp.float32))
    return flat.reshape(count_q, cand)


def shards(queries, codes, quant_rows, row_scale, candidates, shortlist, edges):
    count_rows = codes.shape[0]
    width = quant_rows.shape[1]
    total = count_rows * lax.axis_size("corpus")
    base = lax.axis_index("corpus") * count_rows
    every = lax.all_gather(queries, ("corpus", "batch"), axis=0, tiled=True)
    lists, lengths = (
        lax.all_gather(candidates, ("corpus", "batch"), axis=0, tiled=True),
        lax.all_gather(shortlist, ("corpus", "batch"), axis=0, tiled=True),
    )
    span = count_rows // lax.axis_size("batch")
    first = lax.axis_index("batch") * span
    own_codes = lax.dynamic_slice_in_dim(codes, first, span, 0)
    counts = histogram(every, own_codes, edges, width)
    scores = rescore(every, quant_rows, row_scale, lists, lengths, base, first, span)
    counts, scores = (
        lax.psum_scatter(counts, ("corpus", "batch"), scatter_dimension=0, tiled=True),
        lax.psum_scatter(scores, ("corpus", "batch"), scatter_dimension=0, tiled=True),
    )
    nbins = edges.shape[0] - 1
    hist = counts * (nbins / total)
    return (hist, scores)


def solution(mesh):
    return jax.shard_map(
        shards,
        mesh=mesh,
        in_specs=(
            P(("corpus", "batch"), None),
            P("corpus", None),
            P("corpus", None),
            P("corpus"),
            P(("corpus", "batch"), None),
            P(("corpus", "batch")),
            P(),
        ),
        out_specs=(P(("corpus", "batch"), None), P(("corpus", "batch"), None)),
        check_vma=False,
    )
```

profile of v0, /device:TPU:0, one launch (start us, length us, event | category | flops | bytes accessed | tf_op | source)
XLA Modules:
  0.0 254.0 jit_solution(11925215523051765266)
XLA Ops:
  0.7 43.8 %all-gather.1 = s32[32,4,40]{2,1,0:T(4,128)S(1)} all-gather(s32[1,4,40]{2,1,0:T(4,128)} %bitcast.157), channel_id=1, replica_groups=mesh['corpus'=16,'batch'=2] {'corpus','batch'}, dimensions={0}, use_global_device_ids=true | all-gather | bytes 21120 | tf_op jit(solution)/shard_map/all_gather | solution.py:85
  44.5 0.9 dynamic-update-slice
  45.4 36.8 %all-reduce = s32[128]{0:T(128)S(1)} all-reduce(s32[128]{0:T(128)S(1)} %dynamic-update-slice), channel_id=1, replica_groups=mesh['corpus'=16,'batch'=2] {'corpus','batch'}, use_global_device_ids=true, to_apply=%add | all-reduce | flops 128 | bytes 1024
  82.3 0.6 convert_reduce_fusion.17
  83.7 0.3 reduce-window.9
  84.5 19.3 %scatter_custom_fusion.1 = s32[5632]{0:T(1024)S(1)} fusion(s32[5120]{0:T(1024)S(1)} %bitcast.138, s32[5120]{0:T(1024)S(1)} %iota.22, s32[]{:T(128)} %constant.146.clone.1), kind=kCustom, calls=%fused_computation.56 | custom fusion | bytes 22532 | tf_op jit(solution)/shard_map/scatter | solution.py:56
  104.0 41.8 %all-gather = f32[32,4,1024]{2,1,0:T(4,128)S(1)} all-gather(f32[1,4,1024]{2,1,0:T(4,128)} %bitcast.139), channel_id=1, replica_groups=mesh['corpus'=16,'batch'=2] {'corpus','batch'}, dimensions={0}, use_global_device_ids=true | all-gather | bytes 540672 | tf_op jit(solution)/shard_map/all_gather | solution.py:83
  145.8 0.2 reshape.157
  146.0 22.9 %while.26 = (s32[]{:T(128)}, f32[5120]{0:T(1024)S(1)}, s32[]{:T(128)}, s32[]{:T(128)}, s32[5632]{0:T(1024)S(1)}, /*index=5*/f32[128,1024]{1,0:T(8,128)S(1)}, s32...) while((s32[]{:T(128)}, f32[5120]{0:T(1024)S(1)}, ...), condition=%wide.region_27.28_spmd.clone, body=%wide.region_24.27_spmd.clone.sunk | while | flops 1587718 | bytes 9500855 | solution.py:74
  146.1 0.7 compare_select_fusion.7
  146.8 3.1 %gather_fusion.1 = s32[512]{0:T(512)S(1)} fusion(s32[5120]{0:T(1024)S(1)} %get-tuple-element.558, s32[1024]{0:T(1024)S(1)} %get-tuple-element.455), kind=kCustom, calls=%fused_computation.1.clone.clone.1 | custom fusion | bytes 6144 | tf_op jit(solution)/shard_map/while/body/gather | solution.py:66
  150.0 9.7 %gather_fusion.2 = bf16[512,1024]{1,0:T(8,128)(2,1)} fusion(bf16[6144,1024]{1,0:T(8,128)(2,1)} %get-tuple-element.559, s32[1024]{0:T(1024)S(1)} %pad_clamp_fusion.6), kind=kCustom, calls=%fused_computation.2.clone.clone.1 | custom fusion | bytes 2099200 | tf_op jit(solution)/shard_map/while/body/gather | solution.py:68
  159.7 1.9 gather_fusion
  161.6 1.5 multiply_reduce_fusion.2
  163.1 3.1 %gather_fusion.3 = f32[512]{0:T(512)S(1)} fusion(f32[6144]{0:T(1024)S(1)} %get-tuple-element.560, s32[1024]{0:T(1024)S(1)} %pad_clamp_fusion.6), kind=kCustom, calls=%fused_computation.3.clone.clone.1 | custom fusion | bytes 6144 | tf_op jit(solution)/shard_map/while/body/gather | solution.py:69
  166.2 2.5 scatter_fusion
  169.2 45.6 %while.27 = (s32[]{:T(128)}, f32[128,17]{0,1:T(8,128)S(1)}, s32[3]{0:T(128)S(1)}, s32[3072,32]{0,1:T(8,128)S(1)}, bf16[128,1024]{1,0:T(8,128)(2,1)S(1)}, /*index...) while((s32[]{:T(128)}, f32[128,17]{0,1:T(8,128)S(1)}, s32[3]{0:T(128)S(1)}, ...), condition=%wide.region_18.19_spmd.clone, body=%wide.region_0.18_spmd.clone.sunk | while | flops 280627328 | bytes 4918649 | solution.py:37
  169.2 0.6 dynamic_slice.36
  170.5 0.8 fusion.24
  171.4 0.7 fusion.23
  172.1 12.2 %convert_reduce_fusion.19 = (f32[128]{0:T(128)S(1)}, f32[128]{0:T(128)S(1)}, f32[128]{0:T(128)S(1)}, f32[128]{0:T(128)S(1)}, f32[128]{0:T(128)S(1)}, /*index=5*/...) fusion(f32[]{:T(128)} %bitcast.99, ...), kind=kOutput, calls=%fused_computation.28.clone.1 | convolution fusion | flops 275380096 | bytes 2368068 | tf_op jit(solution)/shard_map/while/body/eval_jaxpr/dot_general | solution.py:25
  184.4 0.6 dynamic_slice.36
  185.7 0.8 fusion.24
  186.6 0.7 fusion.23
  187.3 12.2 %convert_reduce_fusion.19 = (f32[128]{0:T(128)S(1)}, f32[128]{0:T(128)S(1)}, f32[128]{0:T(128)S(1)}, f32[128]{0:T(128)S(1)}, f32[128]{0:T(128)S(1)}, /*index=5*/...) fusion(f32[]{:T(128)} %bitcast.99, ...), kind=kOutput, calls=%fused_computation.28.clone.1 | convolution fusion | flops 275380096 | bytes 2368068 | tf_op jit(solution)/shard_map/while/body/eval_jaxpr/dot_general | solution.py:25
  199.6 0.6 dynamic_slice.36
  200.9 0.8 fusion.24
  201.8 0.7 fusion.23
  202.5 12.2 %convert_reduce_fusion.19 = (f32[128]{0:T(128)S(1)}, f32[128]{0:T(128)S(1)}, f32[128]{0:T(128)S(1)}, f32[128]{0:T(128)S(1)}, f32[128]{0:T(128)S(1)}, /*index=5*/...) fusion(f32[]{:T(128)} %bitcast.99, ...), kind=kOutput, calls=%fused_computation.28.clone.1 | convolution fusion | flops 275380096 | bytes 2368068 | tf_op jit(solution)/shard_map/while/body/eval_jaxpr/dot_general | solution.py:25
  214.9 37.9 %all-reduce.3 = (f32[128,16]{1,0:T(8,128)S(1)}, f32[128,40]{1,0:T(8,128)S(1)}) all-reduce(f32[128,16]{1,0:T(8,128)S(1)} %copy.16, f32[128,40]{1,0:T(8,128)S(1)} %reshape.101), channel_id=2, replica_groups=mesh['corpus'=16,'batch'=2] {'corpus','batch'}, use_global_device_ids=true, to_apply=%region_19.20.clone | all-reduce | flops 7168 | bytes 57344
  252.8 0.6 constant_dynamic-slice_fusion.1
  253.4 0.6 dynamic-slice_multiply_fusion
  (47 shorter events, 1.7 us)
Async XLA Ops:
  0.6 168.4 %copy-start = (s32[6144,32]{0,1:T(8,128)S(1)}, s32[6144,32]{0,1:T(8,128)}, u32[]{:S(2)}) copy-start(s32[6144,32]{0,1:T(8,128)} %param.12) | copy-start | bytes 2359300
  0.6 145.4 %copy-start.1 = (f32[6144]{0:T(1024)S(1)}, f32[6144]{0:T(1024)}, u32[]{:S(2)}) copy-start(f32[6144]{0:T(1024)} %param.14) | copy-start | bytes 73732
  146.0 23.1 %copy-start.2 = (s32[17]{0:T(128)S(1)}, s32[17]{0:T(128)}, u32[]{:S(2)}) copy-start(s32[17]{0:T(128)} %param.17) | copy-start | bytes 208
where the time goes:
time: 256 us; the launch traced here: 254 us
  blocking collectives  160 us (62%)
  local copies, waits for them, and re-layouts  46.4 us (18%)
  matrix products  36.6 us (14%)
  other arithmetic  6.64 us (3%)
    unnamed x2, blocking collectives  74.7 us
    all_gather x1, blocking collectives, shards(): lax.all_gather(candidates, ('corpus', 'batch'), axis=0, tiled=True)  43.8 us
    all_gather x1, blocking collectives, shards(): every = lax.all_gather(queries, ('corpus', 'batch'), axis=0, tiled=True)  41.8 us
    dot_general x3, matrix products, step(): inner = jnp.dot(signs, plus.T, preferred_element_type=jnp.float32)  36.6 us
    scatter x1, local copies, waits for them, and re-layouts, rescore(): order = jnp.zeros((total_slots + group,), jnp.int32).at[place].set(jnp.ar...  19.3 us
    gather x1, local copies, waits for them, and re-layouts, visit(): quant_rows[target].astype(jnp.float32)  9.68 us

commit v1 on v0

v1 whole, which is shorter than its diff:
```python
import functools

import jax
import jax.numpy as jnp
from jax import lax
from jax.experimental import pallas as pl
from jax.experimental.pallas import tpu as pltpu
from jax.sharding import PartitionSpec as P

LANES = 128
HIST_AT = 64


def grid_of(n):
    side = 1
    while 2 * side**3 < n:
        side += 1
    return (n // (side * side), side, side) if 2 * side**3 == n else (n, 1, 1)


def kernel(
    n, cores, queries, cands, lens, edges, scale, codes_hbm, quant_hbm,
    hist_out, scores_out,
    own, gathered, words, quant, plus, flat, split, signs, marks, part, part_out, part_in,
    words_sem, quant_sem, send_sem, recv_sem, out_sem, in_sem,
):
    zs, ys, xs = grid_of(n)
    chip, core = lax.axis_index("corpus"), lax.axis_index("batch")
    me = chip * cores + core
    rows_q, width = queries.shape
    total = n * cores
    span = quant.shape[0]
    count_k = edges.shape[0]
    chunk = quant.shape[0] // quant_sem.shape[0]
    first = core * span

    words_copy = pltpu.make_async_copy(
        codes_hbm.at[:, pl.ds(pl.multiple_of(first, LANES), span)], words, words_sem
    )
    words_copy.start()

    def quant_copy(i):
        at = pl.multiple_of(first + i * chunk, chunk)
        to = pl.multiple_of(i * chunk, chunk)
        return pltpu.make_async_copy(
            quant_hbm.at[pl.ds(at, chunk)], quant.at[pl.ds(to, chunk)], quant_sem.at[i]
        )

    for i in range(quant_sem.shape[0]):
        quant_copy(i).start()

    own[:, :width] = queries[...]
    row = lax.broadcasted_iota(jnp.int32, cands.shape, 0)
    slot = lax.broadcasted_iota(jnp.int32, cands.shape, 1)
    length = jnp.zeros(cands.shape, jnp.int32)
    for i in range(rows_q):
        length = jnp.where(row == i, lens[i], length)
    own[:, width:] = jnp.full((rows_q, LANES), -1.0, jnp.float32)
    own[:, width : width + cands.shape[1]] = jnp.where(
        slot < length, cands[...], -1
    ).astype(jnp.float32)

    z, y, x = chip // (ys * xs), (chip // xs) % ys, chip % xs
    even = core % 2 == 0
    stride_b = jnp.where(even, xs, 1)
    stride_c = jnp.where(even, 1, xs)
    b, c = jnp.where(even, y, x), jnp.where(even, x, y)
    bs, cs = ys, xs

    def chip_at(zz, bb, cc):
        return zz * (ys * xs) + bb * stride_b + cc * stride_c

    barrier = pltpu.get_barrier_semaphore()
    peers = []
    for i in range(1, zs):
        peers.append((chip_at((z + i) % zs, b, c), core))
    for i in range(1, bs):
        peers.append((chip_at(z, (b + i) % bs, c), core))
    for i in range(1, cs):
        peers.append((chip_at(z, b, (c + i) % cs), core))
    for i in range(1, cores):
        peers.append((chip, (core + i) % cores))
    for to in peers:
        pl.semaphore_signal(barrier, inc=1, device_id=to, device_id_type=pl.DeviceIdType.MESH)
    pl.semaphore_wait(barrier, len(peers))
    n_peers = len(peers)
    to_z, to_b = zs - 1, bs - 1
    to_c = cs - 1

    def block_copy(block, kind, to, mine=False):
        return pltpu.make_async_remote_copy(
            src_ref=own if mine else gathered.at[block],
            dst_ref=gathered.at[block],
            send_sem=send_sem.at[kind],
            recv_sem=recv_sem.at[block],
            device_id=to,
            device_id_type=pl.DeviceIdType.MESH,
        )

    def got(block):
        pltpu.make_async_copy(gathered.at[block], gathered.at[block], recv_sem.at[block]).wait()

    def pass_on(block, lo, mine=False):
        for kind in range(lo, n_peers):
            block_copy(block, kind, peers[kind], mine).start()

    def block_z(i):
        return chip_at((z + i) % zs, b, c) * cores + core

    def block_b(i):
        return chip_at((z + i % zs) % zs, (b + 1 + i // zs) % bs, c) * cores + core

    def block_c(i):
        return (
            chip_at((z + i % zs) % zs, (b + (i // zs) % bs) % bs, (c + 1 + i // (zs * bs)) % cs) * cores
            + core
        )

    def block_d(i):
        return (i % n) * cores + (core + 1 + i // n) % cores

    def sent():
        counts = [1] * to_z + [zs] * to_b + [zs * bs] * to_c + [n] * (cores - 1)
        for kind, count in enumerate(counts):
            some = gathered.at[pl.ds(0, count)]
            pltpu.make_async_copy(some, some, send_sem.at[kind]).wait()

    count_b, count_c, count_d = zs * to_b, zs * bs * to_c, n * (cores - 1)
    at_b, at_c, at_d = to_z, to_z + to_b, to_z + to_b + to_c

    def loop(lo, hi, body):
        def step(i, carry):
            body(i)
            return carry

        lax.fori_loop(lo, hi, step, 0)

    bit = lax.broadcasted_iota(jnp.int32, (32, span // 2), 0)

    def unpack(lo, hi):
        def step(w):
            for half in range(2):
                cols = slice(half * (span // 2), (half + 1) * (span // 2))
                word = jnp.broadcast_to(words[pl.ds(w, 1), cols], bit.shape)
                bits = jnp.bitwise_and(lax.shift_right_logical(word, bit), 1)
                plus[pl.ds(pl.multiple_of(w * 32, 32), 32), cols] = bits.astype(
                    jnp.float32
                ).astype(jnp.bfloat16)

        loop(lo, hi, step)

    count_w = words.shape[0]
    cut = [count_w * i // 4 for i in range(5)]

    pass_on(me, 0, True)
    gathered[me] = own[...]
    words_copy.wait()
    unpack(cut[0], cut[1])

    def relay(block_of, lo, start=0):
        def step(i):
            block = block_of(i)
            got(block)
            pass_on(block, lo)

        return step

    loop(1, zs, relay(block_z, at_b))
    unpack(cut[1], cut[2])
    loop(0, count_b, relay(block_b, at_c))
    unpack(cut[2], cut[3])
    loop(0, count_c, relay(block_c, at_d))
    unpack(cut[3], cut[4])
    loop(0, count_d, lambda i: got(block_d(i)))

    def lay(i):
        pair = jnp.concatenate([gathered[2 * i], gathered[2 * i + 1]], axis=0)
        flat[pl.ds(pl.multiple_of(i * 2 * rows_q, 2 * rows_q), 2 * rows_q), :] = pair

    loop(0, total // 2, lay)
    for i in range(quant_sem.shape[0]):
        quant_copy(i).wait()

    tile_q = marks.shape[1]
    groups = span // chunk
    base = (chip * cores + core) * span
    limits = [(edges[k] - width // 2).astype(jnp.float32).astype(jnp.bfloat16) for k in range(count_k)]

    def tile(t):
        q_at = pl.multiple_of(t * tile_q, tile_q)
        vecs = flat[pl.ds(q_at, tile_q), :width]
        index = flat[pl.ds(q_at, tile_q), width:].astype(jnp.int32) - base
        high = vecs.astype(jnp.bfloat16)
        split[:tile_q] = high
        split[tile_q:] = (vecs - high.astype(jnp.float32)).astype(jnp.bfloat16)
        sign = jnp.where(vecs >= 0, 1.0, -1.0)
        signs[...] = sign.astype(jnp.bfloat16)
        half_sum = jnp.sum(sign, axis=1, keepdims=True) * 0.5
        lane = jnp.bitwise_and(index, LANES - 1)
        where = lax.shift_right_arithmetic(index, 7)
        marks[...] = jnp.zeros_like(marks)
        part[...] = jnp.zeros_like(part)

        def step(g):
            r_at = pl.multiple_of(g * chunk, chunk)
            dots = jnp.dot(signs[...], plus[:, pl.ds(r_at, chunk)], preferred_element_type=jnp.float32)
            ham = (half_sum - dots).astype(jnp.bfloat16)
            one = jnp.ones((tile_q, LANES), jnp.bfloat16)
            for k in range(count_k):
                mark = marks[k]
                for j in range(chunk // LANES):
                    piece = ham[:, j * LANES : (j + 1) * LANES]
                    mark = mark + jnp.where(piece >= limits[k], one, jnp.zeros_like(one))
                marks[k] = mark
            both = lax.dot_general(
                split[...], quant[pl.ds(r_at, chunk), :], (((1,), (1,)), ((), ())),
                preferred_element_type=jnp.float32,
            )
            raw = both[:tile_q] + both[tile_q:]
            score = part[...]
            for j in range(chunk // LANES):
                row_at = core * (span // LANES) + g * (chunk // LANES) + j
                piece = raw[:, j * LANES : (j + 1) * LANES] * scale[pl.ds(row_at, 1), :]
                picked = jnp.take_along_axis(piece, lane, axis=1, mode="promise_in_bounds")
                score = jnp.where(where == g * (chunk // LANES) + j, picked, score)
            part[...] = score

        loop(0, groups, step)
        columns = lax.broadcasted_iota(jnp.int32, (LANES, LANES), 1)
        result = part[...]
        for k in range(count_k):
            spot = jnp.where(columns == HIST_AT + k, 1.0, 0.0).astype(jnp.bfloat16)
            result = result + jnp.dot(marks[k], spot, preferred_element_type=jnp.float32)
        per = tile_q // rows_q
        for i in range(per):
            part_out[t * per + i] = result[i * rows_q : (i + 1) * rows_q]

    loop(0, flat.shape[0] // tile_q, tile)

    def result_copy(i):
        to = (me + i) % total
        return pltpu.make_async_remote_copy(
            src_ref=part_out.at[to],
            dst_ref=part_in.at[me],
            send_sem=out_sem,
            recv_sem=in_sem.at[me],
            device_id=(to // cores, to % cores),
            device_id_type=pl.DeviceIdType.MESH,
        )

    loop(1, total, lambda i: result_copy(i).start())
    part_in[me] = part_out[me]

    def wait_in(i):
        source = (me + i) % total
        pltpu.make_async_copy(part_in.at[source], part_in.at[source], in_sem.at[source]).wait()

    loop(1, total, wait_in)
    summed = jnp.sum(part_in[...], axis=0)
    bins = count_k - 1
    above = summed[:, HIST_AT : HIST_AT + bins] - summed[:, HIST_AT + 1 : HIST_AT + 1 + bins]
    hist_out[...] = above * (bins / (total * span))
    scores_out[...] = summed[:, : cands.shape[1]]

    rest = part_in.at[pl.ds(0, total - 1)]
    pltpu.make_async_copy(rest, rest, out_sem).wait()
    sent()


def shards(n, cores, queries, codes, quant_rows, row_scale, candidates, shortlist, edges):
    rows_q, width = queries.shape
    count_rows, count_w = codes.shape
    span = count_rows // cores
    total = n * cores
    tile_q = 128
    chunk = 512
    vmem, smem, hbm = pltpu.VMEM, pltpu.SMEM, pl.ANY
    zs, ys, xs = grid_of(n)
    n_peers = zs + ys + xs + cores - 4
    f32, bf16 = jnp.float32, jnp.bfloat16
    spec = pl.BlockSpec
    return pl.pallas_call(
        functools.partial(kernel, n, cores),
        out_shape=(
            jax.ShapeDtypeStruct((rows_q, edges.shape[0] - 1), f32),
            jax.ShapeDtypeStruct(candidates.shape, f32),
        ),
        in_specs=[
            spec(memory_space=vmem), spec(memory_space=vmem), spec(memory_space=smem),
            spec(memory_space=smem), spec(memory_space=vmem), spec(memory_space=hbm),
            spec(memory_space=hbm),
        ],
        out_specs=(spec(memory_space=vmem), spec(memory_space=vmem)),
        scratch_shapes=[
            vmem((rows_q, width + LANES), f32),
            vmem((total, rows_q, width + LANES), f32),
            vmem((count_w, span), jnp.int32),
            vmem((span, width), bf16),
            vmem((width, span), bf16),
            vmem((total * rows_q, width + LANES), f32),
            vmem((2 * tile_q, width), bf16),
            vmem((tile_q, width), bf16),
            vmem((edges.shape[0], tile_q, LANES), bf16),
            vmem((tile_q, LANES), f32),
            vmem((total, rows_q, LANES), f32),
            vmem((total, rows_q, LANES), f32),
            pltpu.SemaphoreType.DMA,
            pltpu.SemaphoreType.DMA((span // chunk,)),
            pltpu.SemaphoreType.DMA((n_peers,)),
            pltpu.SemaphoreType.DMA((total,)),
            pltpu.SemaphoreType.DMA,
            pltpu.SemaphoreType.DMA((total,)),
        ],
        compiler_params=pltpu.CompilerParams(
            collective_id=0, has_side_effects=True, vmem_limit_bytes=60 * 1024 * 1024
        ),
        name="search",
    )(
        queries, candidates, shortlist, edges,
        row_scale.reshape(count_rows // LANES, LANES), codes.T, quant_rows,
    )


def solution(mesh):
    return jax.shard_map(
        functools.partial(shards, mesh.shape["corpus"], mesh.shape["batch"]),
        mesh=mesh,
        in_specs=(
            P(("corpus", "batch"), None),
            P("corpus", None),
            P("corpus", None),
            P("corpus"),
            P(("corpus", "batch"), None),
            P(("corpus", "batch")),
            P(),
        ),
        out_specs=(P(("corpus", "batch"), None), P(("corpus", "batch"), None)),
        check_vma=False,
    )
```

time: 256 us -> 34.6 us (0.14)
  blocking collectives: 160 us -> 0 us
  local copies, waits for them, and re-layouts: 46.4 us -> 2.48 us
  matrix products: 36.6 us -> 0 us
  Pallas kernels: 0 us -> 31.3 us
  other arithmetic: 6.64 us -> 0 us
    all_gather x2 -> x0, blocking collectives: 85.7 us -> none  [the longest x1 43.8 us: shards(): lax.all_gather(candidates, ('corpus', 'batch'), axis=0, tiled=True)]
    unnamed x2 -> x0, blocking collectives: 74.7 us -> none
    dot_general x3 -> x0, matrix products: 36.6 us -> none  [step(): inner = jnp.dot(signs, plus.T, preferred_element_type=jnp.float32)]
    pallas_call x0 -> x1, Pallas kernels: none -> 31.3 us  [shards(): pl.pallas_call(functools.partial(kernel, n, cores), out_shape=(jax.ShapeD...]
    scatter x2 -> x0, local copies, waits for them, and re-layouts: 21.8 us -> none  [the longest x1 19.3 us: rescore(): order = jnp.zeros((total_slots + group,), jnp.int32).at[place].set(jnp.ar...]
    gather x4 -> x0, local copies, waits for them, and re-layouts: 17.9 us -> none  [the longest x1 9.68 us: visit(): quant_rows[target].astype(jnp.float32)]
    convert_element_type x6 -> x0, other arithmetic: 2.58 us -> none  [the longest x3 2.44 us: unpack(): return signed.astype(jnp.bfloat16)]
where the time goes in v1:
time: 34.6 us; the launch traced here: 34.4 us
  Pallas kernels  31.3 us (90%)
  local copies, waits for them, and re-layouts  2.48 us (7%)
  between operations  0.64 us (2%)
    pallas_call x1, Pallas kernels, shards(): pl.pallas_call(functools.partial(kernel, n, cores), out_shape=(jax.ShapeD...  31.3 us
    unnamed x2, local copies, waits for them, and re-layouts  2.48 us

profile of v1, /device:TPU:0, one launch (start us, length us, event | category | flops | bytes accessed | tf_op | source)
XLA Modules:
  0.0 34.4 jit_solution(12317386803628834244)
XLA Ops:
  0.6 31.3 %search.1 = (f32[4,16]{1,0:T(4,128)}, f32[4,40]{1,0:T(4,128)}) custom-call(f32[4,1024]{1,0:T(4,128)} %queries.1, s32[4,40]{1,0:T(4,128)} %cands.1, s32[4]{0:T(128)} %lens.1, s32[17]{0:T(128)} %edges.1, f32[48,128]{1,0:T(8,128)} %bitcast.3, s32[32,6144]{1,0:T(8,128)} %bitcast.2, bf16[6144,1024]{1,0:T(8,128)(2,1)} %quant_hbm.1), custom_call_target="tpu_custom_call" | custom-call | tf_op jit(solution)/shard_map/search/pallas_call | solution.py:282
  31.9 1.2 %copy.11 = f32[4,16]{1,0:T(4,128)} copy(f32[4,16]{1,0:T(4,128)} %get-tuple-element.4) | data formatting | bytes 512
  33.2 1.2 %copy.12 = f32[4,40]{1,0:T(4,128)} copy(f32[4,40]{1,0:T(4,128)} %get-tuple-element.5) | data formatting | bytes 1280

commit v2 on v1

--- a/solution.py
+++ b/solution.py
@@ -19,10 +19,10 @@
 
 
 def kernel(
-    n, cores, queries, cands, lens, edges, scale, codes_hbm, quant_hbm,
-    hist_out, scores_out,
-    own, gathered, words, quant, plus, flat, split, signs, marks, part, part_out, part_in,
-    words_sem, quant_sem, send_sem, recv_sem, out_sem, in_sem,
+    n, cores, queries_hbm, cands_hbm, lens_hbm, edges_hbm, scale_hbm, codes_hbm, quant_hbm,
+    out,
+    queries, cands, lens, edges, scale, own, gathered, words, quant, plus, flat, split, signs, marks, part, ham_a, ham_b, raw_a, raw_b, part_out, part_in,
+    small_sem, words_sem, quant_sem, send_sem, recv_sem, out_sem, in_sem,
 ):
     zs, ys, xs = grid_of(n)
     chip, core = lax.axis_index("corpus"), lax.axis_index("batch")
@@ -33,32 +33,6 @@
     count_k = edges.shape[0]
     chunk = quant.shape[0] // quant_sem.shape[0]
     first = core * span
-
-    words_copy = pltpu.make_async_copy(
-        codes_hbm.at[:, pl.ds(pl.multiple_of(first, LANES), span)], words, words_sem
-    )
-    words_copy.start()
-
-    def quant_copy(i):
-        at = pl.multiple_of(first + i * chunk, chunk)
-        to = pl.multiple_of(i * chunk, chunk)
-        return pltpu.make_async_copy(
-            quant_hbm.at[pl.ds(at, chunk)], quant.at[pl.ds(to, chunk)], quant_sem.at[i]
-        )
-
-    for i in range(quant_sem.shape[0]):
-        quant_copy(i).start()
-
-    own[:, :width] = queries[...]
-    row = lax.broadcasted_iota(jnp.int32, cands.shape, 0)
-    slot = lax.broadcasted_iota(jnp.int32, cands.shape, 1)
-    length = jnp.zeros(cands.shape, jnp.int32)
-    for i in range(rows_q):
-        length = jnp.where(row == i, lens[i], length)
-    own[:, width:] = jnp.full((rows_q, LANES), -1.0, jnp.float32)
-    own[:, width : width + cands.shape[1]] = jnp.where(
-        slot < length, cands[...], -1
-    ).astype(jnp.float32)
 
     z, y, x = chip // (ys * xs), (chip // xs) % ys, chip % xs
     even = core % 2 == 0
@@ -82,6 +56,47 @@
         peers.append((chip, (core + i) % cores))
     for to in peers:
         pl.semaphore_signal(barrier, inc=1, device_id=to, device_id_type=pl.DeviceIdType.MESH)
+    smalls = [
+        pltpu.make_async_copy(source, target, small_sem.at[i])
+        for i, (source, target) in enumerate(
+            (
+                (queries_hbm, queries), (cands_hbm, cands), (lens_hbm, lens),
+                (edges_hbm, edges), (scale_hbm, scale),
+            )
+        )
+    ]
+    for copy in smalls:
+        copy.start()
+
+    words_copy = pltpu.make_async_copy(
+        codes_hbm.at[:, pl.ds(pl.multiple_of(first, LANES), span)], words, words_sem
+    )
+    words_copy.start()
+
+    def quant_copy(i):
+        at = pl.multiple_of(first + i * chunk, chunk)
+        to = pl.multiple_of(i * chunk, chunk)
+        return pltpu.make_async_copy(
+            quant_hbm.at[pl.ds(at, chunk)], quant.at[pl.ds(to, chunk)], quant_sem.at[i]
+        )
+
+    for i in range(quant_sem.shape[0]):
+        quant_copy(i).start()
+
+    for copy in smalls:
+        copy.wait()
+
+    own[:, :width] = queries[...]
+    row = lax.broadcasted_iota(jnp.int32, cands.shape, 0)
+    slot = lax.broadcasted_iota(jnp.int32, cands.shape, 1)
+    length = jnp.zeros(cands.shape, jnp.int32)
+    for i in range(rows_q):
+        length = jnp.where(row == i, lens[i], length)
+    own[:, width:] = jnp.full((rows_q, LANES), -1.0, jnp.float32)
+    own[:, width : width + cands.shape[1]] = jnp.where(
+        slot < length, cands[...], -1
+    ).astype(jnp.float32)
+
     pl.semaphore_wait(barrier, len(peers))
     n_peers = len(peers)
     to_z, to_b = zs - 1, bs - 1
@@ -104,17 +119,24 @@
         for kind in range(lo, n_peers):
             block_copy(block, kind, peers[kind], mine).start()
 
-    def block_z(i):
-        return chip_at((z + i) % zs, b, c) * cores + core
+    both_sides = jnp.minimum(z, zs - 1 - z)
+    far_side = jnp.where(z < zs - 1 - z, 1, -1)
+
+    def z_at(p):
+        near = p <= 2 * both_sides
+        away = jnp.where(near, (p + 1) // 2, p - both_sides)
+        side = jnp.where(near, 2 * (p % 2) - 1, far_side)
+        return z + away * side
+
+    def block_z(p):
+        return chip_at(z_at(p), b, c) * cores + core
 
     def block_b(i):
-        return chip_at((z + i % zs) % zs, (b + 1 + i // zs) % bs, c) * cores + core
+        return chip_at(z_at(i % zs), (b + 1 + i // zs) % bs, c) * cores + core
 
     def block_c(i):
-        return (
-            chip_at((z + i % zs) % zs, (b + (i // zs) % bs) % bs, (c + 1 + i // (zs * bs)) % cs) * cores
-            + core
-        )
+        to = (c + 1 + i // (zs * bs)) % cs
+        return chip_at(z_at(i % zs), (b + (i // zs) % bs) % bs, to) * cores + core
 
     def block_d(i):
         return (i % n) * cores + (core + 1 + i // n) % cores
@@ -165,9 +187,11 @@
 
         return step
 
-    loop(1, zs, relay(block_z, at_b))
+    loop(1, min(2, zs), relay(block_z, at_b))
+    loop(0, to_b, lambda i: relay(block_b, at_c)(i * zs))
+    loop(min(2, zs), zs, relay(block_z, at_b))
     unpack(cut[1], cut[2])
-    loop(0, count_b, relay(block_b, at_c))
+    loop(0, to_b * (zs - 1), lambda i: relay(block_b, at_c)(i // (zs - 1) * zs + 1 + i % (zs - 1)))
     unpack(cut[2], cut[3])
     loop(0, count_c, relay(block_c, at_d))
     unpack(cut[3], cut[4])
@@ -182,7 +206,8 @@
         quant_copy(i).wait()
 
     tile_q = marks.shape[1]
-    groups = span // chunk
+    unit = ham_a.shape[1]
+    groups = span // unit
     base = (chip * cores + core) * span
     limits = [(edges[k] - width // 2).astype(jnp.float32).astype(jnp.bfloat16) for k in range(count_k)]
 
@@ -201,31 +226,43 @@
         marks[...] = jnp.zeros_like(marks)
         part[...] = jnp.zeros_like(part)
 
-        def step(g):
-            r_at = pl.multiple_of(g * chunk, chunk)
-            dots = jnp.dot(signs[...], plus[:, pl.ds(r_at, chunk)], preferred_element_type=jnp.float32)
-            ham = (half_sum - dots).astype(jnp.bfloat16)
+        def multiply(g, ham, raw):
+            r_at = pl.multiple_of(g * unit, unit)
+            dots = jnp.dot(signs[...], plus[:, pl.ds(r_at, unit)], preferred_element_type=jnp.float32)
+            ham[...] = (half_sum - dots).astype(jnp.bfloat16)
+            both = lax.dot_general(
+                split[...], quant[pl.ds(r_at, unit), :], (((1,), (1,)), ((), ())),
+                preferred_element_type=jnp.float32,
+            )
+            raw[...] = both[:tile_q] + both[tile_q:]
+
+        def collect(g, ham, raw):
             one = jnp.ones((tile_q, LANES), jnp.bfloat16)
             for k in range(count_k):
                 mark = marks[k]
-                for j in range(chunk // LANES):
+                for j in range(unit // LANES):
                     piece = ham[:, j * LANES : (j + 1) * LANES]
                     mark = mark + jnp.where(piece >= limits[k], one, jnp.zeros_like(one))
                 marks[k] = mark
-            both = lax.dot_general(
-                split[...], quant[pl.ds(r_at, chunk), :], (((1,), (1,)), ((), ())),
-                preferred_element_type=jnp.float32,
-            )
-            raw = both[:tile_q] + both[tile_q:]
             score = part[...]
-            for j in range(chunk // LANES):
-                row_at = core * (span // LANES) + g * (chunk // LANES) + j
+            for j in range(unit // LANES):
+                row_at = core * (span // LANES) + g * (unit // LANES) + j
                 piece = raw[:, j * LANES : (j + 1) * LANES] * scale[pl.ds(row_at, 1), :]
                 picked = jnp.take_along_axis(piece, lane, axis=1, mode="promise_in_bounds")
-                score = jnp.where(where == g * (chunk // LANES) + j, picked, score)
+                score = jnp.where(where == g * (unit // LANES) + j, picked, score)
             part[...] = score
 
-        loop(0, groups, step)
+        def step(p):
+            multiply(2 * p + 1, ham_b, raw_b)
+            collect(2 * p, ham_a, raw_a)
+            multiply(2 * p + 2, ham_a, raw_a)
+            collect(2 * p + 1, ham_b, raw_b)
+
+        multiply(0, ham_a, raw_a)
+        loop(0, groups // 2 - 1, step)
+        multiply(groups - 1, ham_b, raw_b)
+        collect(groups - 2, ham_a, raw_a)
+        collect(groups - 1, ham_b, raw_b)
         columns = lax.broadcasted_iota(jnp.int32, (LANES, LANES), 1)
         result = part[...]
         for k in range(count_k):
@@ -259,12 +296,17 @@
     summed = jnp.sum(part_in[...], axis=0)
     bins = count_k - 1
     above = summed[:, HIST_AT : HIST_AT + bins] - summed[:, HIST_AT + 1 : HIST_AT + 1 + bins]
-    hist_out[...] = above * (bins / (total * span))
-    scores_out[...] = summed[:, : cands.shape[1]]
+    out[:, HIST_AT : HIST_AT + bins] = above * (bins / (total * span))
+    out[:, : cands.shape[1]] = summed[:, : cands.shape[1]]
 
     rest = part_in.at[pl.ds(0, total - 1)]
     pltpu.make_async_copy(rest, rest, out_sem).wait()
     sent()
+
+
+def finish(rows, hist, scores):
+    hist[...] = rows[:, HIST_AT : HIST_AT + hist.shape[1]]
+    scores[...] = rows[:, : scores.shape[1]]
 
 
 def shards(n, cores, queries, codes, quant_rows, row_scale, candidates, shortlist, edges):
@@ -274,24 +316,25 @@
     total = n * cores
     tile_q = 128
     chunk = 512
+    unit = 512
     vmem, smem, hbm = pltpu.VMEM, pltpu.SMEM, pl.ANY
     zs, ys, xs = grid_of(n)
     n_peers = zs + ys + xs + cores - 4
     f32, bf16 = jnp.float32, jnp.bfloat16
     spec = pl.BlockSpec
-    return pl.pallas_call(
+    rows = pl.pallas_call(
         functools.partial(kernel, n, cores),
-        out_shape=(
-            jax.ShapeDtypeStruct((rows_q, edges.shape[0] - 1), f32),
-            jax.ShapeDtypeStruct(candidates.shape, f32),
-        ),
+        out_shape=jax.ShapeDtypeStruct((rows_q, LANES), f32),
         in_specs=[
-            spec(memory_space=vmem), spec(memory_space=vmem), spec(memory_space=smem),
-            spec(memory_space=smem), spec(memory_space=vmem), spec(memory_space=hbm),
-            spec(memory_space=hbm),
+            spec(memory_space=hbm) for _ in range(7)
         ],
-        out_specs=(spec(memory_space=vmem), spec(memory_space=vmem)),
+        out_specs=spec(memory_space=vmem),
         scratch_shapes=[
+            vmem(queries.shape, f32),
+            vmem(candidates.shape, jnp.int32),
+            smem(shortlist.shape, jnp.int32),
+            smem(edges.shape, jnp.int32),
+            vmem((count_rows // LANES, LANES), f32),
             vmem((rows_q, width + LANES), f32),
             vmem((total, rows_q, width + LANES), f32),
             vmem((count_w, span), jnp.int32),
@@ -302,8 +345,13 @@
             vmem((tile_q, width), bf16),
             vmem((edges.shape[0], tile_q, LANES), bf16),
             vmem((tile_q, LANES), f32),
+            vmem((tile_q, unit), bf16),
+            vmem((tile_q, unit), bf16),
+            vmem((tile_q, unit), f32),
+            vmem((tile_q, unit), f32),
             vmem((total, rows_q, LANES), f32),
             vmem((total, rows_q, LANES), f32),
+            pltpu.SemaphoreType.DMA((5,)),
             pltpu.SemaphoreType.DMA,
             pltpu.SemaphoreType.DMA((span // chunk,)),
             pltpu.SemaphoreType.DMA((n_peers,)),
@@ -319,6 +367,16 @@
         queries, candidates, shortlist, edges,
         row_scale.reshape(count_rows // LANES, LANES), codes.T, quant_rows,
     )
+    return pl.pallas_call(
+        finish,
+        out_shape=(
+            jax.ShapeDtypeStruct((rows_q, edges.shape[0] - 1), f32),
+            jax.ShapeDtypeStruct(candidates.shape, f32),
+        ),
+        in_specs=[spec(memory_space=vmem)],
+        out_specs=(spec(memory_space=vmem), spec(memory_space=vmem)),
+        name="finish",
+    )(rows)
 
 
 def solution(mesh):

time: 34.6 us -> 30.7 us (0.89)
  local copies, waits for them, and re-layouts: 2.48 us -> 0 us
  Pallas kernels: 31.3 us -> 29.9 us
    unnamed x2 -> x0, local copies, waits for them, and re-layouts: 2.48 us -> none
    pallas_call x1 -> x2, Pallas kernels: 31.3 us -> 29.9 us  [the longest x1 28.5 us: shards(): pl.pallas_call(functools.partial(kernel, n, cores), out_shape=jax.ShapeDt...]
where the time goes in v2:
time: 30.7 us; the launch traced here: 30.5 us
  Pallas kernels  29.9 us (97%)
  between operations  0.64 us (2%)
    pallas_call x1, Pallas kernels, shards(): pl.pallas_call(functools.partial(kernel, n, cores), out_shape=jax.ShapeDt...  28.5 us
    pallas_call x1, Pallas kernels, shards(): pl.pallas_call(finish, out_shape=(jax.ShapeDtypeStruct((rows_q, edges.sha...  1.33 us

profile of v2, /device:TPU:0, one launch (start us, length us, event | category | flops | bytes accessed | tf_op | source)
XLA Modules:
  0.0 30.5 jit_solution(10686474915864549237)
XLA Ops:
  0.6 28.5 %search.1.rows = f32[4,128]{1,0:T(4,128)} custom-call(f32[4,1024]{1,0:T(4,128)} %queries_hbm.1, s32[4,40]{1,0:T(4,128)} %cands_hbm.1, s32[4]{0:T(128)} %lens_hbm.1, s32[17]{0:T(128)} %edges_hbm.1, f32[48,128]{1,0:T(8,128)} %bitcast.3, s32[32,6144]{1,0:T(8,128)} %bitcast.2, bf16[6144,1024]{1,0:T(8,128)(2,1)} %quant_hbm.1), custom_call_target="tpu_custom_call" | custom-call | tf_op jit(solution)/shard_map/search/pallas_call | solution.py:325
  29.2 1.3 %finish.1 = (f32[4,16]{1,0:T(4,128)}, f32[4,40]{1,0:T(4,128)}) custom-call(f32[4,128]{1,0:T(4,128)} %search.1.rows), custom_call_target="tpu_custom_call" | custom-call | tf_op jit(solution)/shard_map/finish/pallas_call | solution.py:370

commit v3 on v2

--- a/solution.py
+++ b/solution.py
@@ -167,7 +167,7 @@
                 bits = jnp.bitwise_and(lax.shift_right_logical(word, bit), 1)
                 plus[pl.ds(pl.multiple_of(w * 32, 32), 32), cols] = bits.astype(
                     jnp.float32
-                ).astype(jnp.bfloat16)
+                ).astype(jnp.float8_e4m3fn)
 
         loop(lo, hi, step)
 
@@ -219,7 +219,7 @@
         split[:tile_q] = high
         split[tile_q:] = (vecs - high.astype(jnp.float32)).astype(jnp.bfloat16)
         sign = jnp.where(vecs >= 0, 1.0, -1.0)
-        signs[...] = sign.astype(jnp.bfloat16)
+        signs[...] = sign.astype(jnp.float8_e4m3fn)
         half_sum = jnp.sum(sign, axis=1, keepdims=True) * 0.5
         lane = jnp.bitwise_and(index, LANES - 1)
         where = lax.shift_right_arithmetic(index, 7)
@@ -339,10 +339,10 @@
             vmem((total, rows_q, width + LANES), f32),
             vmem((count_w, span), jnp.int32),
             vmem((span, width), bf16),
-            vmem((width, span), bf16),
+            vmem((width, span), jnp.float8_e4m3fn),
             vmem((total * rows_q, width + LANES), f32),
             vmem((2 * tile_q, width), bf16),
-            vmem((tile_q, width), bf16),
+            vmem((tile_q, width), jnp.float8_e4m3fn),
             vmem((edges.shape[0], tile_q, LANES), bf16),
             vmem((tile_q, LANES), f32),
             vmem((tile_q, unit), bf16),

time: 30.7 us -> 30.2 us (0.984)
  Pallas kernels: 29.9 us -> 29.4 us
    pallas_call x1, Pallas kernels: 28.5 us -> 28.1 us  [shards(): pl.pallas_call(functools.partial(kernel, n, cores), out_shape=jax.ShapeDt...]
where the time goes in v3:
time: 30.2 us; the launch traced here: 30.1 us
  Pallas kernels  29.4 us (97%)
  between operations  0.64 us (2%)
    pallas_call x1, Pallas kernels, shards(): pl.pallas_call(functools.partial(kernel, n, cores), out_shape=jax.ShapeDt...  28.1 us
    pallas_call x1, Pallas kernels, shards(): pl.pallas_call(finish, out_shape=(jax.ShapeDtypeStruct((rows_q, edges.sha...  1.33 us

profile of v3, /device:TPU:0, one launch (start us, length us, event | category | flops | bytes accessed | tf_op | source)
XLA Modules:
  0.0 30.1 jit_solution(10418836299564628747)
XLA Ops:
  0.6 28.1 %search.1.rows = f32[4,128]{1,0:T(4,128)} custom-call(f32[4,1024]{1,0:T(4,128)} %queries_hbm.1, s32[4,40]{1,0:T(4,128)} %cands_hbm.1, s32[4]{0:T(128)} %lens_hbm.1, s32[17]{0:T(128)} %edges_hbm.1, f32[48,128]{1,0:T(8,128)} %bitcast.3, s32[32,6144]{1,0:T(8,128)} %bitcast.2, bf16[6144,1024]{1,0:T(8,128)(2,1)} %quant_hbm.1), custom_call_target="tpu_custom_call" | custom-call | tf_op jit(solution)/shard_map/search/pallas_call | solution.py:325
  28.7 1.3 %finish.1 = (f32[4,16]{1,0:T(4,128)}, f32[4,40]{1,0:T(4,128)}) custom-call(f32[4,128]{1,0:T(4,128)} %search.1.rows), custom_call_target="tpu_custom_call" | custom-call | tf_op jit(solution)/shard_map/finish/pallas_call | solution.py:370
